TPU v7x, 32 devices: a whole 2x2x4 slice. The times are simulated.
32 devices in a mesh: grp: 2 (over y), seq: 8 (over z, x), head: 2 (over core).
Axes of the slice: x: 2, y: 2, z: 4, core: 2. Of those that a mesh axis runs over, the one named last changes fastest.
Arguments:
- key_cache: bfloat16 [4, 64, 128, 1024], P('grp', ('seq', 'head')), parts along dimension 0, may hold values from -160 to 160, as said below
- value_cache: bfloat16 [4, 64, 128, 1024], P('grp', ('seq', 'head')), parts along dimension 0, may hold values from -16 to 16, as said below
- query: bfloat16 [4, 4096], P('grp', 'head'), parts along dimension 0, may hold values from -48 to 48, as said below
- lengths: int32 [4], P('grp'), parts along dimension 0, may hold values from 128 to 8192, as said below
- block_map: int32 [4, 64], P('grp'), parts along dimension 0, may hold values from 0 to 63, each once within a row
Outputs:
- attended: bfloat16 [4, 4096], P('grp', 'head'), parts along dimension 0
There are 2 independent parts, one for each index of `grp`. A program takes and returns all parts, laid end to end along the dimension named above; each array names one. Nothing has to cross between parts.
Inputs may be any that keep to these rules, and one draw needn't show every extreme that they name: `lengths`: every length is a multiple of 128; in every draw some request has length 8192. `key_cache`: finite entries, drawn afresh for every request, block, token and channel. `value_cache`: finite entries, drawn afresh for every request, block, token and channel. `query`: finite entries, drawn afresh for every request, head and channel.
All inputs are finite; a program needn't handle non-finite values.
Results may differ from a plain program's by a relative error of at most 0.0055.
Values may be sent and summed in bfloat16 or wider, within the bound.
A program may use at most 64 MiB of HBM per device.

v0:
```python
import jax
import jax.numpy as jnp
from jax import lax
from jax.sharding import PartitionSpec as P

QH = 32
KVH = 8
HD = 128
BLK = 128


def rescaled(local, top_all):
    factor = jnp.exp(local[0] - top_all)
    return (local[1] * factor, local[2] * factor[..., None])


def partials(key_rows, value_rows, queries, live_blocks):
    batch_rows = key_rows.shape[0]
    slot_count = key_rows.shape[1]
    group_count = key_rows.shape[3] // HD
    token_count = slot_count * BLK
    key_flat = key_rows.reshape(batch_rows, token_count, group_count, HD)
    value_flat = value_rows.reshape(batch_rows, token_count, group_count, HD)
    query_heads = queries.reshape(batch_rows, group_count, QH // KVH, HD)
    logit_scores = jnp.einsum(
        "bgqd,btgd->bgqt", query_heads, key_flat, preferred_element_type=jnp.float32
    )
    logit_scores = logit_scores * (1.0 / HD**0.5)
    logit_scores = logit_scores.reshape(batch_rows, group_count, QH // KVH, slot_count, BLK)
    live_mask = live_blocks[:, None, None, :, None]
    row_top = jnp.max(jnp.where(live_mask, logit_scores, jnp.float32(-1e30)), axis=(3, 4))
    expo = jnp.where(live_mask, jnp.exp(logit_scores - row_top[..., None, None]), jnp.float32(0.0))
    total = jnp.sum(expo, axis=(3, 4))
    weights = expo.astype(jnp.bfloat16).reshape(batch_rows, group_count, QH // KVH, token_count)
    summed_values = jnp.einsum(
        "bgqt,btgd->bgqd", weights, value_flat, preferred_element_type=jnp.float32
    )
    return (row_top, total, summed_values)


def owned_live(block_map, lengths, position, count):
    owned_blocks = lax.dynamic_slice_in_dim(block_map, position * count, count, 1)
    return owned_blocks < (lengths // BLK)[:, None]


def on_device(key_cache, value_cache, query, lengths, block_map):
    batch_rows = key_cache.shape[0]
    width_here = query.shape[1]
    key_rows, value_rows = (
        lax.all_to_all(key_cache, "head", split_axis=3, concat_axis=1, tiled=True),
        lax.all_to_all(value_cache, "head", split_axis=3, concat_axis=1, tiled=True),
    )
    live_blocks = owned_live(block_map, lengths, lax.axis_index("seq"), key_rows.shape[1])
    local = partials(key_rows, value_rows, query, live_blocks)
    top_every = lax.pmax(local[0], "seq")
    total, summed_values = lax.psum(rescaled(local, top_every), "seq")
    result = summed_values / total[..., None]
    return result.reshape(batch_rows, width_here).astype(jnp.bfloat16)


def solution(mesh):
    placed = (
        P("grp", ("seq", "head"), None, None),
        P("grp", ("seq", "head"), None, None),
        P("grp", "head"),
        P("grp"),
        P("grp", None),
    )
    return jax.shard_map(
        on_device, mesh=mesh, in_specs=placed, out_specs=P("grp", "head"), check_vma=False
    )
```

profile of v0, /device:TPU:0, one launch (start us, length us, event | category | flops | bytes accessed | tf_op | source)
XLA Modules:
  0.0 88.1 jit_solution(8158900298736535543)
XLA Ops:
  0.0 4.3 %copy.10 = bf16[2,4,128,1024]{2,1,0,3:T(4,128)(2,1)} copy(bf16[2,4,128,1024]{3,2,1,0:T(8,128)(2,1)} %param.5) | data formatting | bytes 4194304 | tf_op args[0]
  4.3 0.0 copy-start.2
  4.3 0.0 copy-start.1
  4.3 0.0 copy-start
  4.3 3.9 %all-to-all-start = ((bf16[2,4,128,1024]{2,1,0,3:T(4,128)(2,1)}), bf16[2,4,128,1024]{2,1,0,3:T(4,128)(2,1)S(1)}, u32[]{:S(2)}, u32[]{:S(2)}) async-start(bf16[2,4,128,1024]{2,1,0,3:T(4,128)(2,1)} %copy.10), calls=%async_computation | async-start | bytes 4194304 | tf_op jit(solution)/shard_map/all_to_all | solution.py:50
  8.2 0.0 copy-done.2
  8.3 0.0 copy-done.1
  8.3 0.1 dynamic-slice_compare_fusion
  8.3 0.1 broadcast_bitcast_fusion
  8.4 0.0 copy-done
  8.5 4.3 %copy.13 = bf16[2,4,128,1024]{2,1,0,3:T(4,128)(2,1)} copy(bf16[2,4,128,1024]{3,2,1,0:T(8,128)(2,1)} %param.6) | data formatting | bytes 4194304 | tf_op args[1]
  12.8 0.0 all-to-all-done
  12.8 4.8 %all-to-all-start.1 = ((bf16[2,4,128,1024]{2,1,0,3:T(4,128)(2,1)}), bf16[2,4,128,1024]{2,1,0,3:T(4,128)(2,1)}, u32[]{:S(2)}, u32[]{:S(2)}) async-start(bf16[2,4,128,1024]{2,1,0,3:T(4,128)(2,1)} %copy.13), calls=%async_computation.1 | async-start | bytes 4194304 | tf_op jit(solution)/shard_map/all_to_all | solution.py:51
  17.6 3.0 %copy.11 = bf16[2,4,128,2,512]{4,2,1,3,0:T(8,128)(2,1)} copy(bf16[2,4,128,2,512]{2,1,0,4,3:T(4,128)(2,1)S(1)} %bitcast.19) | data formatting | bytes 4194304 | tf_op jit(solution)/shard_map/all_to_all | solution.py:50
  20.6 2.5 %reshape.24 = bf16[2,1024,4,128]{3,2,1,0:T(4,128)(2,1)S(1)} reshape(bf16[2,2,4,128,512]{4,3,2,1,0:T(8,128)(2,1)} %bitcast.20) | data formatting | bytes 4194304 | tf_op jit(solution)/shard_map/reshape | solution.py:22
  23.2 0.7 select_reduce_fusion
  23.9 23.1 %pmax.7 = f32[2,4,4]{2,1,0:T(4,128)S(1)} all-reduce(f32[2,4,4]{2,1,0:T(4,128)S(1)} %get-tuple-element.9), channel_id=1, replica_groups=mesh['grp'=2,'seq'=8,'head'=2] {'seq'}, use_global_device_ids=true, to_apply=%region_1.2 | all-reduce | flops 32 | bytes 256 | tf_op jit(solution)/shard_map/pmax | solution.py:55
  47.0 0.2 fusion.10
  47.3 0.0 all-to-all-done.1
  47.3 3.0 %copy.14 = bf16[2,4,128,2,512]{4,2,1,3,0:T(8,128)(2,1)S(1)} copy(bf16[2,4,128,2,512]{2,1,0,4,3:T(4,128)(2,1)} %bitcast.2) | data formatting | bytes 4194304 | tf_op jit(solution)/shard_map/all_to_all | solution.py:51
  50.2 2.1 %reshape.25 = bf16[2,1024,4,128]{3,2,1,0:T(4,128)(2,1)} reshape(bf16[2,2,4,128,512]{4,3,2,1,0:T(8,128)(2,1)S(1)} %bitcast.21) | data formatting | bytes 4194304 | tf_op jit(solution)/shard_map/reshape | solution.py:23
  52.3 2.0 %fusion.7 = f32[2,4,4,128]{3,2,1,0:T(4,128)S(1)} fusion(bf16[2,1024,4,128]{3,2,1,0:T(4,128)(2,1)} %reshape.25, f32[2,4,4,1024]{3,2,1,0:T(4,128)S(1)} %get-tuple-element.10, f32[2,4,4]{2,1,0:T(4,128)S(1)} %get-tuple-element.9, pred[2,1024]{1,0:T(4,128)(4,1)S(1)} %bitcast.27, f32[2,4,4]{2,1,0:T(4,128)S(1)} %bitcast.29), kind=kOutput, calls=%fused_computation.5 | convolution fusion | flops 8491008 | bytes 2246912 | tf_op jit(solution)/shard_map/bgqt,btgd->bgqd/dot_general | solution.py:35
  54.4 33.0 %all-reduce = (f32[2,4,4,128]{3,2,1,0:T(4,128)S(1)}, f32[2,4,4]{2,1,0:T(4,128)S(1)}) all-reduce(f32[2,4,4,128]{3,2,1,0:T(4,128)S(1)} %fusion.7, f32[2,4,4]{2,1,0:T(4,128)S(1)} %bitcast.24), channel_id=1, replica_groups=mesh['grp'=2,'seq'=8,'head'=2] {'seq'}, use_global_device_ids=true, to_apply=%region_2.3 | all-reduce | flops 4128 | bytes 33024 | tf_op jit(solution)/shard_map/psum | solution.py:56
  87.4 0.1 divide_convert_fusion
  87.5 0.6 convert_element_type.12
  (4 shorter events, 0.0 us)
Async XLA Ops:
  4.3 3.9 %copy-start.2 = (s32[2]{0:T(128)S(1)}, s32[2]{0:T(128)}, u32[]{:S(2)}) copy-start(s32[2]{0:T(128)} %param.8) | copy-start | bytes 28
  4.3 3.9 %copy-start.1 = (s32[2,64]{1,0:T(2,128)S(1)}, s32[2,64]{1,0:T(2,128)}, u32[]{:S(2)}) copy-start(s32[2,64]{1,0:T(2,128)} %param.9) | copy-start | bytes 1540
  4.3 4.1 %copy-start = (bf16[2,2048]{1,0:T(2,128)(2,1)S(1)}, bf16[2,2048]{1,0:T(2,128)(2,1)}, u32[]{:S(2)}) copy-start(bf16[2,2048]{1,0:T(2,128)(2,1)} %param.7) | copy-start | bytes 24580
  4.3 8.5 %all-to-all-start = ((bf16[2,4,128,1024]{2,1,0,3:T(4,128)(2,1)}), bf16[2,4,128,1024]{2,1,0,3:T(4,128)(2,1)S(1)}, u32[]{:S(2)}, u32[]{:S(2)}) async-start(bf16[2,4,128,1024]{2,1,0,3:T(4,128)(2,1)} %copy.10), calls=%async_computation | async-start | bytes 4194304 | tf_op jit(solution)/shard_map/all_to_all | solution.py:50
  12.8 34.5 %all-to-all-start.1 = ((bf16[2,4,128,1024]{2,1,0,3:T(4,128)(2,1)}), bf16[2,4,128,1024]{2,1,0,3:T(4,128)(2,1)}, u32[]{:S(2)}, u32[]{:S(2)}) async-start(bf16[2,4,128,1024]{2,1,0,3:T(4,128)(2,1)} %copy.13), calls=%async_computation.1 | async-start | bytes 4194304 | tf_op jit(solution)/shard_map/all_to_all | solution.py:51
where the time goes:
time: 88.7 us; the launch traced here: 88.1 us
  blocking collectives  56.2 us (63%)
  local copies, waits for them, and re-layouts  20 us (23%)
  starting transfers between devices  8.72 us (10%)
  matrix products  2.79 us (3%)
    psum x1, blocking collectives, on_device(): total, summed_values = lax.psum(rescaled(local, top_every), 'seq')  33 us
    pmax x1, blocking collectives, on_device(): top_every = lax.pmax(local[0], 'seq')  23.1 us
    unnamed x10, local copies, waits for them, and re-layouts  8.71 us
    all_to_all x1, starting transfers between devices, on_device(): lax.all_to_all(value_cache, 'head', split_axis=3, concat_axis=1, tiled=True)  4.82 us
    all_to_all x1, starting transfers between devices, on_device(): lax.all_to_all(key_cache, 'head', split_axis=3, concat_axis=1, tiled=True)  3.9 us
    all_to_all x1, local copies, waits for them, and re-layouts, on_device(): lax.all_to_all(key_cache, 'head', split_axis=3, concat_axis=1, tiled=True)  3.04 us
    all_to_all x1, local copies, waits for them, and re-layouts, on_device(): lax.all_to_all(value_cache, 'head', split_axis=3, concat_axis=1, tiled=True)  2.97 us
    reshape x1, local copies, waits for them, and re-layouts, partials(): key_flat = key_rows.reshape(batch_rows, token_count, group_count, HD)  2.55 us
  transfers between devices with their start and end apart: 2, of which 0 were waited for; matrix products, arithmetic and copies ran while one was open for 13% of the time, Pallas kernels for 0%

commit v1 on v0

--- a/solution.py
+++ b/solution.py
@@ -7,6 +7,13 @@
 KVH = 8
 HD = 128
 BLK = 128
+
+
+def exchange_blocks(block, axis, split, join):
+    size = lax.axis_size(axis)
+    blocks = jnp.stack(jnp.split(block, size, axis=split), axis=0)
+    blocks = lax.all_to_all(blocks, axis, split_axis=0, concat_axis=0)
+    return jnp.concatenate(blocks, axis=join)
 
 
 def rescaled(local, top_all):
@@ -47,7 +54,7 @@
     batch_rows = key_cache.shape[0]
     width_here = query.shape[1]
     key_rows, value_rows = (
-        lax.all_to_all(key_cache, "head", split_axis=3, concat_axis=1, tiled=True),
+        exchange_blocks(key_cache, "head", 3, 1),
         lax.all_to_all(value_cache, "head", split_axis=3, concat_axis=1, tiled=True),
     )
     live_blocks = owned_live(block_map, lengths, lax.axis_index("seq"), key_rows.shape[1])

time: 88.7 us -> 86.1 us (0.971)
  local copies, waits for them, and re-layouts: 20 us -> 15.9 us
  other arithmetic: 0.39 us -> 1.86 us
    unnamed x10 -> x9, local copies, waits for them, and re-layouts: 8.71 us -> 4.4 us
    another operation x0 -> x2, local copies, waits for them, and re-layouts: none -> 4.3 us  [the longest x1 2.56 us: partials(): key_flat = key_rows.reshape(batch_rows, token_count, group_count, HD)]
    all_to_all x1 -> x0, local copies, waits for them, and re-layouts: 3.04 us -> none  [on_device(): lax.all_to_all(key_cache, 'head', split_axis=3, concat_axis=1, tiled=True)]
    another operation x0 -> x1, other arithmetic: none -> 1.48 us  [exchange_blocks(): blocks = jnp.stack(jnp.split(block, size, axis=split), axis=0)]
    reshape x1, local copies, waits for them, and re-layouts: 2.55 us -> 1.54 us  [exchange_blocks(): return jnp.concatenate(blocks, axis=join)]
  transfers between devices with their start and end apart: 2 -> 2, of which waited for: 0 -> 0; matrix products, arithmetic and copies ran while one was open for 13% -> 11% of each run, Pallas kernels for 0% -> 0%
where the time goes in v1:
time: 86.1 us; the launch traced here: 85.5 us
  blocking collectives  56.2 us (65%)
  local copies, waits for them, and re-layouts  15.9 us (18%)
  starting transfers between devices  8.71 us (10%)
  matrix products  2.79 us (3%)
  other arithmetic  1.86 us (2%)
    psum x1, blocking collectives, on_device(): total, summed_values = lax.psum(rescaled(local, top_every), 'seq')  33 us
    pmax x1, blocking collectives, on_device(): top_every = lax.pmax(local[0], 'seq')  23.1 us
    all_to_all x1, starting transfers between devices, on_device(): lax.all_to_all(value_cache, 'head', split_axis=3, concat_axis=1, tiled=True)  4.82 us
    unnamed x9, local copies, waits for them, and re-layouts  4.4 us
    all_to_all x1, starting transfers between devices, exchange_blocks(): blocks = lax.all_to_all(blocks, axis, split_axis=0, concat_axis=0)  3.89 us
    all_to_all x1, local copies, waits for them, and re-layouts, on_device(): lax.all_to_all(value_cache, 'head', split_axis=3, concat_axis=1, tiled=True)  2.97 us
    another operation x1, local copies, waits for them, and re-layouts, partials(): key_flat = key_rows.reshape(batch_rows, token_count, group_count, HD)  2.56 us
    reshape x1, local copies, waits for them, and re-layouts, partials(): value_flat = value_rows.reshape(batch_rows, token_count, group_count, HD)  2.09 us
  transfers between devices with their start and end apart: 2, of which 0 were waited for; matrix products, arithmetic and copies ran while one was open for 11% of the time, Pallas kernels for 0%

profile of v1, /device:TPU:0, one launch (start us, length us, event | category | flops | bytes accessed | tf_op | source)
XLA Modules:
  0.0 85.5 jit_solution(14250481112158091273)
XLA Ops:
  0.0 1.7 %slice_bitcast_fusion.1 = (bf16[1,2,4,128,512]{4,3,2,1,0:T(8,128)(2,1)S(1)}, bf16[1,2,4,128,512]{4,3,2,1,0:T(8,128)(2,1)S(1)}) fusion(bf16[2,4,128,1024]{3,2,1,0:T(8,128)(2,1)} %param.5), kind=kLoop, calls=%fused_computation.8 | loop fusion | bytes 4194304 | tf_op jit(solution)/shard_map/stack | solution.py:14
  1.7 1.5 %pad_maximum_fusion = bf16[2,2,4,128,512]{4,3,2,1,0:T(8,128)(2,1)} fusion(bf16[1,2,4,128,512]{4,3,2,1,0:T(8,128)(2,1)S(1)} %get-tuple-element.10, bf16[1,2,4,128,512]{4,3,2,1,0:T(8,128)(2,1)S(1)} %get-tuple-element.9), kind=kLoop, calls=%fused_computation | loop fusion | flops 1048576 | bytes 4194304 | tf_op jit(solution)/shard_map/stack | solution.py:14
  3.2 0.0 copy-start.2
  3.2 0.0 copy-start.1
  3.2 3.9 %all-to-all-start = ((bf16[2,2,4,128,512]{4,3,2,1,0:T(8,128)(2,1)}), bf16[2,2,4,128,512]{4,3,2,1,0:T(8,128)(2,1)S(1)}, u32[]{:S(2)}, u32[]{:S(2)}) async-start(bf16[2,2,4,128,512]{4,3,2,1,0:T(8,128)(2,1)} %pad_maximum_fusion), calls=%async_computation | async-start | bytes 4194304 | tf_op jit(solution)/shard_map/all_to_all | solution.py:15
  7.1 0.0 copy-done.2
  7.2 0.0 copy-done.1
  7.2 0.1 dynamic-slice_compare_fusion
  7.3 0.1 broadcast_bitcast_fusion
  7.3 4.3 %copy.12 = bf16[2,4,128,1024]{2,1,0,3:T(4,128)(2,1)} copy(bf16[2,4,128,1024]{3,2,1,0:T(8,128)(2,1)} %param.6) | data formatting | bytes 4194304 | tf_op args[1]
  11.6 0.0 all-to-all-done
  11.6 4.8 %all-to-all-start.1 = ((bf16[2,4,128,1024]{2,1,0,3:T(4,128)(2,1)}), bf16[2,4,128,1024]{2,1,0,3:T(4,128)(2,1)}, u32[]{:S(2)}, u32[]{:S(2)}) async-start(bf16[2,4,128,1024]{2,1,0,3:T(4,128)(2,1)} %copy.12), calls=%async_computation.1 | async-start | bytes 4194304 | tf_op jit(solution)/shard_map/all_to_all | solution.py:58
  16.5 1.5 %copy.10 = bf16[2,2,4,128,512]{4,3,2,1,0:T(8,128)(2,1)} copy(bf16[2,2,4,128,512]{4,3,2,0,1:T(8,128)(2,1)S(1)} %bitcast.26) | data formatting | bytes 4194304 | tf_op jit(solution)/shard_map/reshape | solution.py:16
  18.0 0.0 copy-start
  18.0 2.6 %reshape_reshape.3 = bf16[2,1024,4,128]{3,2,1,0:T(4,128)(2,1)S(1)} reshape(bf16[2,2,4,128,512]{4,3,2,1,0:T(8,128)(2,1)} %copy.10) | data formatting | bytes 4194304 | tf_op jit(solution)/shard_map/reshape;reshape | solution.py:29
  20.6 0.0 copy-done
  20.6 0.7 select_reduce_fusion
  21.3 23.1 %pmax.7 = f32[2,4,4]{2,1,0:T(4,128)S(1)} all-reduce(f32[2,4,4]{2,1,0:T(4,128)S(1)} %get-tuple-element.11), channel_id=1, replica_groups=mesh['grp'=2,'seq'=8,'head'=2] {'seq'}, use_global_device_ids=true, to_apply=%region_1.2 | all-reduce | flops 32 | bytes 256 | tf_op jit(solution)/shard_map/pmax | solution.py:62
  44.5 0.2 bitcast_reduce_fusion
  44.7 0.0 all-to-all-done.1
  44.7 3.0 %copy.13 = bf16[2,4,128,2,512]{4,2,1,3,0:T(8,128)(2,1)S(1)} copy(bf16[2,4,128,2,512]{2,1,0,4,3:T(4,128)(2,1)} %bitcast.4) | data formatting | bytes 4194304 | tf_op jit(solution)/shard_map/all_to_all | solution.py:58
  47.7 2.1 %reshape.24 = bf16[2,1024,4,128]{3,2,1,0:T(4,128)(2,1)} reshape(bf16[2,2,4,128,512]{4,3,2,1,0:T(8,128)(2,1)S(1)} %bitcast.27) | data formatting | bytes 4194304 | tf_op jit(solution)/shard_map/reshape | solution.py:30
  49.8 2.0 %fusion.7 = f32[2,4,4,128]{3,2,1,0:T(4,128)S(1)} fusion(bf16[2,1024,4,128]{3,2,1,0:T(4,128)(2,1)} %reshape.24, f32[2,4,1024,4]{2,3,1,0:T(4,128)S(1)} %get-tuple-element.12, f32[2,4,4]{2,1,0:T(4,128)S(1)} %get-tuple-element.11, pred[2,1024]{1,0:T(4,128)(4,1)S(1)} %bitcast.33, f32[2,4,4]{2,1,0:T(4,128)S(1)} %bitcast.35), kind=kOutput, calls=%fused_computation.6 | convolution fusion | flops 8491008 | bytes 2246912 | tf_op jit(solution)/shard_map/bgqt,btgd->bgqd/dot_general | solution.py:42
  51.8 33.0 %all-reduce = (f32[2,4,4,128]{3,2,1,0:T(4,128)S(1)}, f32[2,4,4]{2,1,0:T(4,128)S(1)}) all-reduce(f32[2,4,4,128]{3,2,1,0:T(4,128)S(1)} %fusion.7, f32[2,4,4]{2,1,0:T(4,128)S(1)} %bitcast.30), channel_id=1, replica_groups=mesh['grp'=2,'seq'=8,'head'=2] {'seq'}, use_global_device_ids=true, to_apply=%region_2.3 | all-reduce | flops 4128 | bytes 33024 | tf_op jit(solution)/shard_map/psum | solution.py:63
  84.8 0.1 divide_convert_fusion
  84.9 0.6 convert_element_type.12
  (4 shorter events, 0.0 us)
Async XLA Ops:
  3.2 3.9 %copy-start.2 = (s32[2]{0:T(128)S(1)}, s32[2]{0:T(128)}, u32[]{:S(2)}) copy-start(s32[2]{0:T(128)} %param.8) | copy-start | bytes 28
  3.2 3.9 %copy-start.1 = (s32[2,64]{1,0:T(2,128)S(1)}, s32[2,64]{1,0:T(2,128)}, u32[]{:S(2)}) copy-start(s32[2,64]{1,0:T(2,128)} %param.9) | copy-start | bytes 1540
  3.2 8.4 %all-to-all-start = ((bf16[2,2,4,128,512]{4,3,2,1,0:T(8,128)(2,1)}), bf16[2,2,4,128,512]{4,3,2,1,0:T(8,128)(2,1)S(1)}, u32[]{:S(2)}, u32[]{:S(2)}) async-start(bf16[2,2,4,128,512]{4,3,2,1,0:T(8,128)(2,1)} %pad_maximum_fusion), calls=%async_computation | async-start | bytes 4194304 | tf_op jit(solution)/shard_map/all_to_all | solution.py:15
  11.6 33.0 %all-to-all-start.1 = ((bf16[2,4,128,1024]{2,1,0,3:T(4,128)(2,1)}), bf16[2,4,128,1024]{2,1,0,3:T(4,128)(2,1)}, u32[]{:S(2)}, u32[]{:S(2)}) async-start(bf16[2,4,128,1024]{2,1,0,3:T(4,128)(2,1)} %copy.12), calls=%async_computation.1 | async-start | bytes 4194304 | tf_op jit(solution)/shard_map/all_to_all | solution.py:58
  18.0 2.6 %copy-start = (bf16[2,2048]{1,0:T(2,128)(2,1)S(1)}, bf16[2,2048]{1,0:T(2,128)(2,1)}, u32[]{:S(2)}) copy-start(bf16[2,2048]{1,0:T(2,128)(2,1)} %param.7) | copy-start | bytes 24580
